TPU v7x, 256 devices: a whole 4x4x8 slice. The times are simulated.
256 devices in a mesh: blk: 128 (over y, z, x_lo, core), rel: 2 (over x_hi).
Axes of the slice: x: 4 (x_hi: 2, x_lo: 2; x = x_hi * 2 + x_lo), y: 4, z: 8, core: 2. Of those that a mesh axis runs over, the one named last changes fastest.
Arguments:
- user_table: float32 [131072, 512], P(('blk', 'rel')), may hold values from -1.5 to 1.5
- user_accum: float32 [131072], P(('blk', 'rel')), may hold values from 1 to 100
- item_table: float32 [262144, 512], P(('blk', 'rel')), may hold values from -1.5 to 1.5
- item_accum: float32 [262144], P(('blk', 'rel')), may hold values from 1 to 100
- relation: bfloat16 [512, 512], replicated, may hold values from -0.25 to 0.25
- relation_accum: float32 [512], replicated, may hold values from 0.5 to 8
- targets: bfloat16 [2, 131072, 2048], P(None, 'blk', 'rel'), may hold values from 0 to 1
Outputs:
- user_table_next: float32 [131072, 512], P(('blk', 'rel'))
- user_accum_next: float32 [131072], P(('blk', 'rel'))
- item_table_next: float32 [262144, 512], P(('blk', 'rel'))
- item_accum_next: float32 [262144], P(('blk', 'rel'))
- relation_step: float32 [512, 512], replicated
- relation_accum_next: float32 [512], replicated
All inputs are finite; a program needn't handle non-finite values.
Results may differ from a plain program's by a relative error of at most 0.0037.
The roundings to bfloat16 on the way count: a program that leaves them out, or rounds other values in their place, can miss the bound.
Values may be sent and summed in bfloat16 or wider, within the bound.
A program may use at most 64 MiB of HBM per device.

v0:
```python
import jax
import jax.numpy as jnp
from jax import lax
from jax.sharding import PartitionSpec as P

learn_rate = 0.1
epsilon = 1e-06


def from_everyone(shard, axis):
    copies = jnp.broadcast_to(shard, (lax.axis_size(axis), *shard.shape))
    return lax.all_to_all(copies, axis, split_axis=0, concat_axis=0, tiled=True)


def in_order(pieces, dim):
    pieces = jnp.moveaxis(pieces, 0, dim)
    dims = pieces.shape
    return pieces.reshape(*dims[:dim], dims[dim] * dims[dim + 1], *dims[dim + 2 :])


def collect(shard, axis, dim):
    pieces = from_everyone(shard, axis)
    return in_order(pieces, dim)


def in_blocks(shard, dim, peers):
    before, after = (shard.shape[:dim], shard.shape[dim + 1 :])
    return jnp.moveaxis(shard.reshape(*before, peers, -1, *after), dim, 0)


def sum_at_owner(shard, axis, dim):
    peers = lax.axis_size(axis)
    pieces = lax.all_to_all(in_blocks(shard, dim, peers), axis, 0, 0, tiled=True)
    return jnp.sum(pieces, axis=0)


def from_behind(shard, axis, by):
    peers = lax.axis_size(axis)
    return lax.ppermute(shard, axis, [(i, (i + by) % peers) for i in range(peers)])


def adagrad_rows(table, accum, grads):
    accum_next = accum + jnp.mean(grads * grads, axis=1)
    return (table - learn_rate * grads * lax.rsqrt(accum_next + epsilon)[:, None], accum_next)


def per_device(user_table, user_accum, item_table, item_accum, relation, relation_accum, targets):
    blocks = lax.axis_size("blk")
    rounds = targets.shape[0]
    users_now, user_sums = (user_table, user_accum)
    items_now, item_sums = (item_table, item_accum)
    relation_local = jnp.zeros((relation.shape[0], relation.shape[1]), jnp.float32)
    for turn in range(rounds):
        whole_users = collect(users_now.astype(jnp.bfloat16), "rel", 0)
        item_bf = items_now.astype(jnp.bfloat16)
        anchor = jnp.dot(whole_users, relation, preferred_element_type=jnp.float32).astype(
            jnp.bfloat16
        )
        scores = lax.dot_general(
            anchor, item_bf, (((1,), (1,)), ((), ())), preferred_element_type=jnp.float32
        )
        errors = (jax.nn.sigmoid(scores) - targets[turn].astype(jnp.float32)).astype(jnp.bfloat16)
        mapped = lax.dot_general(
            item_bf, relation, (((1,), (1,)), ((), ())), preferred_element_type=jnp.float32
        ).astype(jnp.bfloat16)
        user_grad = sum_at_owner(
            jnp.dot(errors, mapped, preferred_element_type=jnp.float32), "rel", 0
        )
        item_grad = lax.dot_general(
            errors, anchor, (((0,), (0,)), ((), ())), preferred_element_type=jnp.float32
        )
        crossed = lax.dot_general(
            whole_users, errors, (((0,), (0,)), ((), ())), preferred_element_type=jnp.float32
        ).astype(jnp.bfloat16)
        term = jnp.dot(crossed, item_bf, preferred_element_type=jnp.float32)
        relation_local = relation_local + term
        users_now, user_sums = adagrad_rows(users_now, user_sums, user_grad)
        items_now, item_sums = adagrad_rows(items_now, item_sums, item_grad)
        items_now, item_sums = from_behind((items_now, item_sums), "blk", 1)
    total = lax.psum(relation_local, ("blk", "rel"))
    mean_grad = total / (blocks * rounds)
    accum_next = relation_accum + jnp.mean(mean_grad * mean_grad, axis=1)
    relation_step = mean_grad * lax.rsqrt(accum_next + epsilon)[:, None]
    return (users_now, user_sums, items_now, item_sums, relation_step, accum_next)


def solution(mesh):
    return jax.shard_map(
        per_device,
        mesh=mesh,
        in_specs=(
            P(("blk", "rel"), None),
            P(("blk", "rel")),
            P(("blk", "rel"), None),
            P(("blk", "rel")),
            P(),
            P(),
            P(None, "blk", "rel"),
        ),
        out_specs=(
            P(("blk", "rel"), None),
            P(("blk", "rel")),
            P(("blk", "rel"), None),
            P(("blk", "rel")),
            P(),
            P(),
        ),
        check_vma=False,
    )
```

profile of v0, /device:TPU:2, one launch (start us, length us, event | category | flops | bytes accessed | tf_op | source)
XLA Modules:
  0.0 427.7 jit_solution(13035519853064472672)
XLA Ops:
  7.2 0.0 copy-start
  7.2 1.4 convert_element_type.49
  8.5 1.0 broadcast_in_dim.4
  9.6 4.5 %all-to-all-start = ((bf16[2,512,512]{2,1,0:T(8,128)(2,1)}), bf16[2,512,512]{2,1,0:T(8,128)(2,1)}, u32[]{:S(2)}, u32[]{:S(2)}) async-start(bf16[2,512,512]{2,1,0:T(8,128)(2,1)} %broadcast_in_dim.4), calls=%async_computation | async-start | bytes 2097152 | tf_op jit(solution)/shard_map/all_to_all | solution.py:12
  14.0 1.9 copy.13
  16.0 13.5 %all-to-all-done = bf16[2,512,512]{2,1,0:T(8,128)(2,1)} async-done(((bf16[2,512,512]{2,1,0:T(8,128)(2,1)}), bf16[2,512,512]{2,1,0:T(8,128)(2,1)}, u32[]{:S(2)}, u32[]{:S(2)}) %all-to-all-start) | async-done | bytes 1048608 | tf_op jit(solution)/shard_map/all_to_all | solution.py:12
  29.5 2.1 convolution_convert_fusion.5
  31.6 3.3 fusion.1
  34.9 0.0 copy-start.7
  34.9 1.3 copy-done.7
  36.2 2.7 multiply_reduce_fusion.1
  38.9 5.4 %fusion.2 = f32[1024,512]{1,0:T(8,128)} fusion(bf16[1024,1024]{1,0:T(8,128)(2,1)} %copy-done.7, bf16[512,512]{1,0:T(8,128)(2,1)S(1)} %copy-done, f32[1024,512]{1,0:T(8,128)} %param.9), kind=kOutput, calls=%fused_computation.20 | convolution fusion | flops 1611661312 | bytes 6815744 | tf_op jit(solution)/shard_map/dot_general | solution.py:67
  44.3 4.9 %all-to-all-start.1 = ((f32[2,512,512]{2,1,0:T(8,128)}), f32[2,512,512]{2,1,0:T(8,128)}, u32[]{:S(2)}, u32[]{:S(2)}) async-start(f32[2,512,512]{2,1,0:T(8,128)} %bitcast.29), calls=%async_computation.1 | async-start | bytes 4194304 | tf_op jit(solution)/shard_map/all_to_all | solution.py:33
  49.3 3.5 multiply_subtract_fusion.1
  52.8 44.8 %all-to-all-done.1 = f32[2,512,512]{2,1,0:T(8,128)} async-done(((f32[2,512,512]{2,1,0:T(8,128)}), f32[2,512,512]{2,1,0:T(8,128)}, u32[]{:S(2)}, u32[]{:S(2)}) %all-to-all-start.1) | async-done | bytes 2097184 | tf_op jit(solution)/shard_map/all_to_all | solution.py:33
  97.6 1.9 reduce_sum.63
  99.4 0.1 multiply_reduce_fusion.4
  99.6 0.2 fusion.5
  99.8 1.0 broadcast_in_dim.5
  100.8 4.4 %all-to-all-start.2 = ((bf16[2,512,512]{2,1,0:T(8,128)(2,1)}), bf16[2,512,512]{2,1,0:T(8,128)(2,1)}, u32[]{:S(2)}, u32[]{:S(2)}) async-start(bf16[2,512,512]{2,1,0:T(8,128)(2,1)} %broadcast_in_dim.5), calls=%async_computation.2 | async-start | bytes 2097152 | tf_op jit(solution)/shard_map/all_to_all | solution.py:12
  105.3 0.0 all-reduce.2.cloned.1.call-start
  105.3 0.3 collective-permute-start.1
  105.6 5.3 %fusion.4 = f32[512,512]{1,0:T(8,128)} fusion(bf16[1024,1024]{1,0:T(8,128)(2,1)} %copy-done.7, bf16[1024,512]{1,0:T(8,128)(2,1)} %bitcast, f32[1024,512]{1,0:T(8,128)} %param.9), kind=kOutput, calls=%fused_computation.22 | convolution fusion | flops 1611661312 | bytes 6291456 | tf_op jit(solution)/shard_map/dot_general | solution.py:75
  110.9 8.1 %all-to-all-done.2 = bf16[2,512,512]{2,1,0:T(8,128)(2,1)} async-done(((bf16[2,512,512]{2,1,0:T(8,128)(2,1)}), bf16[2,512,512]{2,1,0:T(8,128)(2,1)}, u32[]{:S(2)}, u32[]{:S(2)}) %all-to-all-start.2) | async-done | bytes 1048608 | tf_op jit(solution)/shard_map/all_to_all | solution.py:12
  119.1 1.9 convolution_convert_fusion.3
  121.0 0.0 copy-start.6
  121.0 0.9 copy-done.6
  122.0 5.2 %fusion = bf16[1024,1024]{1,0:T(8,128)(2,1)} fusion(bf16[1024,512]{1,0:T(8,128)(2,1)S(1)} %convolution_convert_fusion.3, bf16[2,1024,1024]{2,1,0:T(8,128)(2,1)} %param.13, f32[1024,512]{0,1:T(8,128)} %collective-permute-done), kind=kOutput, calls=%fused_computation.1 | convolution fusion | flops 1080557568 | bytes 7340032 | tf_op jit(solution)/shard_map/dot_general | solution.py:59
  127.2 5.6 %convolution_add_fusion = f32[512,512]{1,0:T(8,128)} fusion(f32[512,512]{1,0:T(8,128)} %fusion.4, bf16[1024,512]{1,0:T(8,128)(2,1)} %bitcast.3, bf16[1024,1024]{1,0:T(8,128)(2,1)} %fusion, f32[1024,512]{0,1:T(8,128)} %collective-permute-done), kind=kOutput, calls=%fused_computation.14 | convolution fusion | flops 1611923456 | bytes 7340032 | tf_op jit(solution)/shard_map/dot_general | solution.py:75
  132.8 4.5 %multiply_reduce_fusion = (f32[1024]{0:T(1024)S(1)}, f32[1024,512]{0,1:T(8,128)}) fusion(bf16[1024,1024]{1,0:T(8,128)(2,1)} %fusion, bf16[1024,512]{1,0:T(8,128)(2,1)} %copy-done.6), kind=kOutput, calls=%fused_computation.5 | convolution fusion | flops 1074789376 | bytes 5246976 | tf_op jit(solution)/shard_map/dot_general | solution.py:69
  137.2 0.0 all-reduce.2.cloned.1.call-update
  137.3 4.2 multiply_subtract_fusion
  141.4 0.0 collective-permute-start.2
  141.4 5.4 %fusion.3 = f32[1024,512]{1,0:T(8,128)} fusion(bf16[1024,1024]{1,0:T(8,128)(2,1)} %fusion, bf16[512,512]{1,0:T(8,128)(2,1)S(1)} %copy-done, f32[1024,512]{0,1:T(8,128)} %collective-permute-done), kind=kOutput, calls=%fused_computation.21 | convolution fusion | flops 1611661312 | bytes 6815744 | tf_op jit(solution)/shard_map/dot_general | solution.py:67
  146.8 5.0 %all-to-all-start.3 = ((f32[2,512,512]{2,1,0:T(8,128)}), f32[2,512,512]{2,1,0:T(8,128)}, u32[]{:S(2)}, u32[]{:S(2)}) async-start(f32[2,512,512]{2,1,0:T(8,128)} %bitcast.28), calls=%async_computation.3 | async-start | bytes 4194304 | tf_op jit(solution)/shard_map/all_to_all | solution.py:33
  151.8 0.1 collective-permute-start.3
  151.9 38.7 %collective-permute-done.3 = f32[1024]{0:T(1024)S(1)} collective-permute-done((f32[1024]{0:T(1024)S(1)}, f32[1024]{0:T(1024)S(1)}, u32[]{:S(2)}, u32[]{:S(2)}) %collective-permute-start.3) | collective-permute-done | bytes 4128 | tf_op jit(solution)/shard_map/ppermute | solution.py:39
  190.7 215.1 %all-reduce.2.cloned.1.call-done = f32[512,512]{1,0:T(8,128)} async-done(((f32[512,512]{1,0:T(8,128)}), f32[512,512]{1,0:T(8,128)}) %all-reduce.2.cloned.1.call-update) | async-done | bytes 1048592 | tf_op jit(solution)/shard_map/psum | solution.py:80
  405.8 1.4 multiply_reduce_fusion.2
  407.2 0.6 rsqrt_multiply_fusion.2
  407.8 2.3 broadcast_multiply_fusion
  410.1 0.0 all-to-all-done.3
  410.1 2.9 reduce_sum.66
  413.0 1.4 multiply_reduce_fusion.3
  414.4 0.6 rsqrt_multiply_fusion.3
  414.9 2.4 multiply_subtract_fusion.2
  417.4 2.9 copy.14
  420.3 0.6 copy.17
  (18 shorter events, 0.1 us)
Async XLA Ops:
  7.2 22.3 %copy-start = (bf16[512,512]{1,0:T(8,128)(2,1)S(1)}, bf16[512,512]{1,0:T(8,128)(2,1)}, u32[]{:S(2)}) copy-start(bf16[512,512]{1,0:T(8,128)(2,1)} %param.11) | copy-start | bytes 1572868
  9.6 19.9 %all-to-all-start = ((bf16[2,512,512]{2,1,0:T(8,128)(2,1)}), bf16[2,512,512]{2,1,0:T(8,128)(2,1)}, u32[]{:S(2)}, u32[]{:S(2)}) async-start(bf16[2,512,512]{2,1,0:T(8,128)(2,1)} %broadcast_in_dim.4), calls=%async_computation | async-start | bytes 2097152 | tf_op jit(solution)/shard_map/all_to_all | solution.py:12
  29.5 2.1 copy-start.2
  34.9 1.3 copy-start.7
  44.3 5.0 %copy-start.4 = (f32[1024]{0:T(1024)S(1)}, f32[1024]{0:T(1024)}, u32[]{:S(2)}) copy-start(f32[1024]{0:T(1024)} %param.10) | copy-start | bytes 12292
  44.3 53.3 %all-to-all-start.1 = ((f32[2,512,512]{2,1,0:T(8,128)}), f32[2,512,512]{2,1,0:T(8,128)}, u32[]{:S(2)}, u32[]{:S(2)}) async-start(f32[2,512,512]{2,1,0:T(8,128)} %bitcast.29), calls=%async_computation.1 | async-start | bytes 4194304 | tf_op jit(solution)/shard_map/all_to_all | solution.py:33
  52.8 46.8 %copy-start.3 = (f32[512]{0:T(512)S(1)}, f32[512]{0:T(512)}, u32[]{:S(2)}) copy-start(f32[512]{0:T(512)} %param.8) | copy-start | bytes 6148
  52.8 46.8 %copy-start.1 = (f32[512,512]{1,0:T(8,128)S(1)}, f32[512,512]{1,0:T(8,128)}, u32[]{:S(2)}) copy-start(f32[512,512]{1,0:T(8,128)} %param.7) | copy-start | bytes 3145732
  52.8 68.2 %collective-permute-start = (f32[1024,512]{0,1:T(8,128)}, f32[1024,512]{0,1:T(8,128)}, u32[]{:S(2)}, u32[]{:S(2)}) collective-permute-start(f32[1024,512]{0,1:T(8,128)} %multiply_subtract_fusion.1), channel_id=1, source_target_pairs={{0,2},{2,4},{4,6},{6,8},{8,10},{10,12},{12,14},{14,16},{16,18},{18... | collective-permute-start | bytes 6291464 | tf_op jit(solution)/shard_map/ppermute | solution.py:39
  100.8 18.2 %all-to-all-start.2 = ((bf16[2,512,512]{2,1,0:T(8,128)(2,1)}), bf16[2,512,512]{2,1,0:T(8,128)(2,1)}, u32[]{:S(2)}, u32[]{:S(2)}) async-start(bf16[2,512,512]{2,1,0:T(8,128)(2,1)} %broadcast_in_dim.5), calls=%async_computation.2 | async-start | bytes 2097152 | tf_op jit(solution)/shard_map/all_to_all | solution.py:12
  105.3 300.5 %all-reduce.2.cloned.1.call-start = ((), (), s32[]{:S(2)}) async-start(), calls=%async_computation.4 | async-start | bytes 2097152 | tf_op jit(solution)/shard_map/psum | solution.py:80
  105.3 31.9 %collective-permute-start.1 = (f32[1024]{0:T(1024)S(1)}, f32[1024]{0:T(1024)S(1)}, u32[]{:S(2)}, u32[]{:S(2)}) collective-permute-start(f32[1024]{0:T(1024)S(1)} %get-tuple-element.19), channel_id=1, source_target_pairs={{0,2},{2,4},{4,6},{6,8},{8,10},{10,12},{12,14},{14,16},{16,18},{18... | collective-permute-start | bytes 12296 | tf_op jit(solution)/shard_map/ppermute | solution.py:39
  121.0 1.0 copy-start.6
  141.4 275.9 %collective-permute-start.2 = (f32[1024,512]{0,1:T(8,128)}, f32[1024,512]{0,1:T(8,128)}, u32[]{:S(2)}, u32[]{:S(2)}) collective-permute-start(f32[1024,512]{0,1:T(8,128)} %multiply_subtract_fusion), channel_id=1, source_target_pairs={{0,2},{2,4},{4,6},{6,8},{8,10},{10,12},{12,14},{14,16},{16,18},{18... | collective-permute-start | bytes 6291464 | tf_op jit(solution)/shard_map/ppermute | solution.py:39
  146.8 260.4 %copy-start.5 = (f32[512]{0:T(512)S(1)}, f32[512]{0:T(512)}, u32[]{:S(2)}) copy-start(f32[512]{0:T(512)} %param.12) | copy-start | bytes 6148
  146.8 263.3 %all-to-all-start.3 = ((f32[2,512,512]{2,1,0:T(8,128)}), f32[2,512,512]{2,1,0:T(8,128)}, u32[]{:S(2)}, u32[]{:S(2)}) async-start(f32[2,512,512]{2,1,0:T(8,128)} %bitcast.28), calls=%async_computation.3 | async-start | bytes 4194304 | tf_op jit(solution)/shard_map/all_to_all | solution.py:33
  151.8 38.8 %collective-permute-start.3 = (f32[1024]{0:T(1024)S(1)}, f32[1024]{0:T(1024)S(1)}, u32[]{:S(2)}, u32[]{:S(2)}) collective-permute-start(f32[1024]{0:T(1024)S(1)} %get-tuple-element.15), channel_id=1, source_target_pairs={{0,2},{2,4},{4,6},{6,8},{8,10},{10,12},{12,14},{14,16},{16,18},{18... | collective-permute-start | bytes 12296 | tf_op jit(solution)/shard_map/ppermute | solution.py:39
Sparse Core Ops, SparseCore 0:
  137.4 268.3 all-reduce.1
where the time goes:
time: 429 us; the launch traced here: 428 us
  waiting for transfers between devices  320 us (75%)
  matrix products  41.4 us (10%)
  other arithmetic  22.8 us (5%)
  starting transfers between devices  19.2 us (4%)
  between operations  14.2 us (3%)
  local copies, waits for them, and re-layouts  9.78 us (2%)
    psum x1, waiting for transfers between devices, per_device(): total = lax.psum(relation_local, ('blk', 'rel'))  215 us
    all_to_all x2, waiting for transfers between devices, sum_at_owner(): lax.all_to_all(in_blocks(shard, dim, peers), axis, 0, 0, tiled=True)  44.8 us
    ppermute x4, waiting for transfers between devices, from_behind(): lax.ppermute(shard, axis, [(i, (i + by) % peers) for i in range(peers)])  38.8 us
    all_to_all x2, waiting for transfers between devices, from_everyone(): return lax.all_to_all(copies, axis, split_axis=0, concat_axis=0, tiled=True)  21.7 us
    dot_general x2, matrix products, per_device(): term = jnp.dot(crossed, item_bf, preferred_element_type=jnp.float32)  10.9 us
    dot_general x2, matrix products, per_device(): jnp.dot(errors, mapped, preferred_element_type=jnp.float32)  10.8 us
    sub x3, other arithmetic, adagrad_rows(): table - learn_rate * grads * lax.rsqrt(accum_next + epsilon)[:, None]  10.1 us
    all_to_all x2, starting transfers between devices, sum_at_owner(): lax.all_to_all(in_blocks(shard, dim, peers), axis, 0, 0, tiled=True)  9.91 us
  transfers between devices with their start and end apart: 9, of which 5 were waited for; matrix products, arithmetic and copies ran while one was open for 12% of the time, Pallas kernels for 0%

commit v1 on v0

--- a/solution.py
+++ b/solution.py
@@ -77,7 +77,8 @@
         users_now, user_sums = adagrad_rows(users_now, user_sums, user_grad)
         items_now, item_sums = adagrad_rows(items_now, item_sums, item_grad)
         items_now, item_sums = from_behind((items_now, item_sums), "blk", 1)
-    total = lax.psum(relation_local, ("blk", "rel"))
+    half = lax.psum(relation_local, "rel")
+    total = lax.psum(half, "blk")
     mean_grad = total / (blocks * rounds)
     accum_next = relation_accum + jnp.mean(mean_grad * mean_grad, axis=1)
     relation_step = mean_grad * lax.rsqrt(accum_next + epsilon)[:, None]

time: 429 us -> 1330 us (3.10)
  waiting for transfers between devices: 320 us -> 1220 us
    psum x1 -> x2, waiting for transfers between devices: 215 us -> 1150 us  [the longest x1 1080 us: per_device(): total = lax.psum(half, 'blk')]
    ppermute x4, waiting for transfers between devices: 38.8 us -> 3.03 us  [from_behind(): lax.ppermute(shard, axis, [(i, (i + by) % peers) for i in range(peers)])]
  transfers between devices with their start and end apart: 9 -> 10, of which waited for: 5 -> 6; matrix products, arithmetic and copies ran while one was open for 12% -> 4% of each run, Pallas kernels for 0% -> 0%
where the time goes in v1:
time: 1330 us
  waiting for transfers between devices  1220 us (92%)
  matrix products  41.4 us (3%)
  other arithmetic  22.8 us (2%)
  starting transfers between devices  19.1 us (1%)
  between operations  14.2 us (1%)
    psum x1, waiting for transfers between devices, per_device(): total = lax.psum(half, 'blk')  1080 us
    psum x1, waiting for transfers between devices, per_device(): half = lax.psum(relation_local, 'rel')  64.1 us
    all_to_all x2, waiting for transfers between devices, sum_at_owner(): lax.all_to_all(in_blocks(shard, dim, peers), axis, 0, 0, tiled=True)  44.8 us
  transfers between devices with their start and end apart: 10, of which 6 were waited for; matrix products, arithmetic and copies ran while one was open for 4% of the time, Pallas kernels for 0%

profile of v1, /device:TPU:2, one launch (start us, length us, event | category | flops | bytes accessed | tf_op | source)
XLA Modules:
  0.0 1325.1 jit_solution(2742707844427058937)
XLA Ops:
  7.2 0.0 copy-start
  7.2 1.4 convert_element_type.49
  8.5 1.0 broadcast_in_dim.4
  9.6 4.5 all-to-all-start
  14.0 1.9 copy.13
  16.0 13.5 %all-to-all-done = bf16[2,512,512]{2,1,0:T(8,128)(2,1)} async-done(((bf16[2,512,512]{2,1,0:T(8,128)(2,1)}), bf16[2,512,512]{2,1,0:T(8,128)(2,1)}, u32[]{:S(2)}, u32[]{:S(2)}) %all-to-all-start) | async-done | bytes 1048608 | tf_op jit(solution)/shard_map/all_to_all | solution.py:12
  29.5 2.1 convolution_convert_fusion.5
  31.6 3.3 fusion.1
  34.9 0.0 copy-start.7
  34.9 1.3 copy-done.7
  36.2 2.7 multiply_reduce_fusion.1
  38.9 5.4 fusion.2
  44.3 4.9 all-to-all-start.1
  49.3 3.5 multiply_subtract_fusion.1
  52.8 44.8 %all-to-all-done.1 = f32[2,512,512]{2,1,0:T(8,128)} async-done(((f32[2,512,512]{2,1,0:T(8,128)}), f32[2,512,512]{2,1,0:T(8,128)}, u32[]{:S(2)}, u32[]{:S(2)}) %all-to-all-start.1) | async-done | bytes 2097184 | tf_op jit(solution)/shard_map/all_to_all | solution.py:33
  97.6 1.9 reduce_sum.63
  99.4 0.1 multiply_reduce_fusion.4
  99.6 0.2 fusion.5
  99.8 1.0 broadcast_in_dim.5
  100.8 4.4 all-to-all-start.2
  105.3 0.0 all-reduce.3.cloned.1.call-start
  105.3 0.3 collective-permute-start.1
  105.6 5.3 fusion.4
  110.9 8.1 all-to-all-done.2
  119.1 1.9 convolution_convert_fusion.3
  121.0 0.9 copy-done.6
  122.0 5.2 fusion
  127.2 5.6 convolution_add_fusion
  132.8 4.5 multiply_reduce_fusion
  137.2 0.0 all-reduce.3.cloned.1.call-update
  137.3 4.2 multiply_subtract_fusion
  141.4 5.4 fusion.3
  146.8 4.8 all-to-all-start.3
  151.7 0.0 all-reduce.5.cloned.1.call-start
  151.7 64.1 %all-reduce.3.cloned.1.call-done = f32[512,512]{1,0:T(8,128)} async-done(((f32[512,512]{1,0:T(8,128)}), f32[512,512]{1,0:T(8,128)}) %all-reduce.3.cloned.1.call-update) | async-done | bytes 1048592 | tf_op jit(solution)/shard_map/psum | solution.py:80
  215.8 0.0 all-reduce.5.cloned.1.call-update
  215.8 0.1 collective-permute-start.3
  215.9 3.0 collective-permute-done.3
  218.9 2.9 reduce_sum.66
  221.8 1.4 multiply_reduce_fusion.3
  223.1 0.6 rsqrt_multiply_fusion.3
  223.7 2.4 multiply_subtract_fusion.2
  226.2 2.9 copy.14
  229.1 1084.3 %all-reduce.5.cloned.1.call-done = f32[512,512]{1,0:T(8,128)} async-done(((f32[512,512]{1,0:T(8,128)}), f32[512,512]{1,0:T(8,128)}) %all-reduce.5.cloned.1.call-update) | async-done | bytes 1048592 | tf_op jit(solution)/shard_map/psum | solution.py:81
  1313.4 1.4 multiply_reduce_fusion.2
  1314.8 0.6 rsqrt_multiply_fusion.2
  1315.4 2.3 broadcast_multiply_fusion
  1317.7 0.6 copy.18
  (21 shorter events, 0.1 us)
Async XLA Ops:
  7.2 22.3 %copy-start = (bf16[512,512]{1,0:T(8,128)(2,1)S(1)}, bf16[512,512]{1,0:T(8,128)(2,1)}, u32[]{:S(2)}) copy-start(bf16[512,512]{1,0:T(8,128)(2,1)} %param.11) | copy-start | bytes 1572868
  9.6 19.9 %all-to-all-start = ((bf16[2,512,512]{2,1,0:T(8,128)(2,1)}), bf16[2,512,512]{2,1,0:T(8,128)(2,1)}, u32[]{:S(2)}, u32[]{:S(2)}) async-start(bf16[2,512,512]{2,1,0:T(8,128)(2,1)} %broadcast_in_dim.4), calls=%async_computation | async-start | bytes 2097152 | tf_op jit(solution)/shard_map/all_to_all | solution.py:12
  29.5 2.1 copy-start.2
  34.9 1.3 copy-start.7
  44.3 5.0 copy-start.4
  44.3 53.3 %all-to-all-start.1 = ((f32[2,512,512]{2,1,0:T(8,128)}), f32[2,512,512]{2,1,0:T(8,128)}, u32[]{:S(2)}, u32[]{:S(2)}) async-start(f32[2,512,512]{2,1,0:T(8,128)} %bitcast.29), calls=%async_computation.1 | async-start | bytes 4194304 | tf_op jit(solution)/shard_map/all_to_all | solution.py:33
  52.8 46.8 %copy-start.3 = (f32[512]{0:T(512)S(1)}, f32[512]{0:T(512)}, u32[]{:S(2)}) copy-start(f32[512]{0:T(512)} %param.8) | copy-start | bytes 6148
  52.8 46.8 %copy-start.1 = (f32[512,512]{1,0:T(8,128)S(1)}, f32[512,512]{1,0:T(8,128)}, u32[]{:S(2)}) copy-start(f32[512,512]{1,0:T(8,128)} %param.7) | copy-start | bytes 3145732
  52.8 68.2 %collective-permute-start = (f32[1024,512]{0,1:T(8,128)}, f32[1024,512]{0,1:T(8,128)}, u32[]{:S(2)}, u32[]{:S(2)}) collective-permute-start(f32[1024,512]{0,1:T(8,128)} %multiply_subtract_fusion.1), channel_id=1, source_target_pairs={{0,2},{2,4},{4,6},{6,8},{8,10},{10,12},{12,14},{14,16},{16,18},{18... | collective-permute-start | bytes 6291464 | tf_op jit(solution)/shard_map/ppermute | solution.py:39
  100.8 18.2 %all-to-all-start.2 = ((bf16[2,512,512]{2,1,0:T(8,128)(2,1)}), bf16[2,512,512]{2,1,0:T(8,128)(2,1)}, u32[]{:S(2)}, u32[]{:S(2)}) async-start(bf16[2,512,512]{2,1,0:T(8,128)(2,1)} %broadcast_in_dim.5), calls=%async_computation.2 | async-start | bytes 2097152 | tf_op jit(solution)/shard_map/all_to_all | solution.py:12
  105.3 110.5 %all-reduce.3.cloned.1.call-start = ((), (), s32[]{:S(2)}) async-start(), calls=%async_computation.4 | async-start | bytes 2097152 | tf_op jit(solution)/shard_map/psum | solution.py:80
  105.3 31.9 %collective-permute-start.1 = (f32[1024]{0:T(1024)S(1)}, f32[1024]{0:T(1024)S(1)}, u32[]{:S(2)}, u32[]{:S(2)}) collective-permute-start(f32[1024]{0:T(1024)S(1)} %get-tuple-element.19), channel_id=1, source_target_pairs={{0,2},{2,4},{4,6},{6,8},{8,10},{10,12},{12,14},{14,16},{16,18},{18... | collective-permute-start | bytes 12296 | tf_op jit(solution)/shard_map/ppermute | solution.py:39
  121.0 1.0 copy-start.6
  141.4 84.7 %collective-permute-start.2 = (f32[1024,512]{0,1:T(8,128)}, f32[1024,512]{0,1:T(8,128)}, u32[]{:S(2)}, u32[]{:S(2)}) collective-permute-start(f32[1024,512]{0,1:T(8,128)} %multiply_subtract_fusion), channel_id=1, source_target_pairs={{0,2},{2,4},{4,6},{6,8},{8,10},{10,12},{12,14},{14,16},{16,18},{18... | collective-permute-start | bytes 6291464 | tf_op jit(solution)/shard_map/ppermute | solution.py:39
  146.8 72.1 %all-to-all-start.3 = ((f32[2,512,512]{2,1,0:T(8,128)}), f32[2,512,512]{2,1,0:T(8,128)}, u32[]{:S(2)}, u32[]{:S(2)}) async-start(f32[2,512,512]{2,1,0:T(8,128)} %bitcast.28), calls=%async_computation.3 | async-start | bytes 4194304 | tf_op jit(solution)/shard_map/all_to_all | solution.py:33
  151.7 1161.7 %all-reduce.5.cloned.1.call-start = ((), (), s32[]{:S(2)}) async-start(), calls=%async_computation.5 | async-start | bytes 2097152 | tf_op jit(solution)/shard_map/psum | solution.py:81
  215.8 3.1 collective-permute-start.3
  226.2 1088.6 %copy-start.5 = (f32[512]{0:T(512)S(1)}, f32[512]{0:T(512)}, u32[]{:S(2)}) copy-start(f32[512]{0:T(512)} %param.12) | copy-start | bytes 6148
Sparse Core Ops, SparseCore 0:
  137.4 78.3 all-reduce.2
  218.4 1094.9 all-reduce.4
